TPU v7x, 128 devices: a whole 4x4x4 slice. The times are simulated.
128 devices in a mesh: gx: 16 (over x_lo, z, core), gy: 8 (over y, x_hi).
Axes of the slice: x: 4 (x_hi: 2, x_lo: 2; x = x_hi * 2 + x_lo), y: 4, z: 4, core: 2. Of those that a mesh axis runs over, the one named last changes fastest.
Arguments:
- right_side: float32 [256, 256, 128], P('gx', 'gy'), may hold values from -6 to 6
- shift: float32 [256, 256, 128], P('gx', 'gy'), may hold values from 0.5 to 8
Outputs:
- solution_field: float32 [256, 256, 128], P('gx', 'gy')
- residual: float32 [256, 256, 128], P('gx', 'gy')
All inputs are finite; a program needn't handle non-finite values.
Results may differ from a plain program's by a relative error of at most 0.0003.
Values sent between devices are 32-bit elements; how exact they have to be, the bound alone decides.
No kernel may reach another device: no remote copies, remote signals or barrier semaphores. Data moves between devices by JAX's collectives and lax.ppermute only.
A program may use at most 128 MiB of HBM per device.

v0:
```python
import jax
import jax.numpy as jnp
from jax import lax
from jax.experimental import pallas as pl
from jax.experimental.pallas import tpu as pltpu
from jax.sharding import PartitionSpec as P


STEP = 0.5
RELAX = 0.7
CENTER = 26.0
AX = ("gx", "gy")
CX, CY, CZ = 16, 32, 128
ROWS = 40
BX = CX + 4
WX = CX + 6
F32 = jnp.float32
IROWS = 80


def place():
    gx, gy = lax.axis_index("gx"), lax.axis_index("gy")
    ends = (gx == 0, gx == lax.axis_size("gx") - 1, gy == 0, gy == lax.axis_size("gy") - 1)
    return [gx & 1, gy & 1] + [jnp.where(end, 1, 0) for end in ends]


def sds(*shape):
    return jax.ShapeDtypeStruct(shape, F32)


def lanes():
    return lax.broadcasted_iota(jnp.int32, (ROWS, CZ), 1)


def rows():
    return lax.broadcasted_iota(jnp.int32, (ROWS, CZ), 0)


def zy_sum(p, sh):
    lane = lanes()
    zs = p + jnp.where(lane >= sh, pltpu.roll(p, sh, 1), 0.0)
    zs = zs + jnp.where(lane < CZ - sh, pltpu.roll(p, CZ - sh, 1), 0.0)
    return zs + pltpu.roll(zs, sh, 0) + pltpu.roll(zs, ROWS - sh, 0)


def band_matrix(terms, sh):
    at = lax.broadcasted_iota(jnp.int32, (terms * CZ, CZ), 0) & (CZ - 1)
    gap = jnp.abs(at - lax.broadcasted_iota(jnp.int32, (terms * CZ, CZ), 1))
    return jnp.where((gap == 0) | (gap == sh), 1.0, 0.0).astype(jnp.bfloat16)


def z_sums(planes, band):
    n = planes.shape[0]
    left = planes.reshape(n * ROWS, CZ)
    terms = []
    for _ in range(band.shape[0] // CZ):
        if terms:
            left = left - terms[-1].astype(F32)
        terms.append(left.astype(jnp.bfloat16))
    sums = jnp.dot(jnp.concatenate(terms, axis=1), band[...], preferred_element_type=F32)
    return sums.reshape(n, ROWS, CZ)


def wide_stencil(n, e, band, emit):
    sums = z_sums(e[...], band)

    def y_sum(x):
        zs = sums[x]
        return zs + pltpu.roll(zs, 1, 0) + pltpu.roll(zs, ROWS - 1, 0)

    prev, cur = None, y_sum(0)
    for x in range(n):
        nxt = y_sum(x + 1) if x + 1 < n else None
        total = cur
        if prev is not None:
            total = total + prev
        if nxt is not None:
            total = total + nxt
        emit(x, total)
        prev, cur = cur, nxt


def stencil(n, sh, load, emit):
    prev = None
    cur = zy_sum(load(0), sh)
    for x in range(n):
        nxt = zy_sum(load(x + 1), sh) if x + 1 < n else None
        total = cur
        if prev is not None:
            total = total + prev
        if nxt is not None:
            total = total + nxt
        emit(x, total)
        prev, cur = cur, nxt


def pair_sum(a, level):
    sh = 2**level
    bit = ((rows() + 7) >> level) & 1
    a = a + jnp.where(bit == 0, pltpu.roll(a, ROWS - sh, 0), pltpu.roll(a, sh, 0))
    bit = (lanes() >> level) & 1
    return a + jnp.where(bit == 0, pltpu.roll(a, CZ - sh, 1), pltpu.roll(a, sh, 1))


def smooth0(n, e, g, w, band):
    def emit(x, total):
        here = e[x]
        e[x] = (1.0 - RELAX) * here + w[x] * (g[x] + (total - here))

    wide_stencil(n, e, band, emit)


def smooth(n, sh, e, g, w):
    def emit(x, total):
        here = e[x]
        e[x] = (1.0 - RELAX) * here + w[x] * (g[x] + (total - here))

    stencil(n, sh, lambda x: e[x], emit)


def restrict(n, level, e, g, dp1, g_next, band=None):
    held = []

    def emit(x, total):
        left = (g[x] + total) - dp1[x] * e[x]
        if x % 2 == 0:
            held.append(left)
        else:
            g_next[x // 2] = 0.5 * pair_sum(held.pop() + left, level)

    if band is None:
        stencil(n, 2**level, lambda x: e[x], emit)
    else:
        wide_stencil(n, e, band, emit)


def vcycle(e0, g0, dp1_0, w0, dp1_1, w1, w2, e1, g1, e2, g2, band):
    n0, n1, n2 = BX, BX // 2, BX // 4
    for x in range(n0):
        e0[x] = w0[x] * g0[x]
    smooth0(n0, e0, g0, w0, band)
    restrict(n0, 0, e0, g0, dp1_0, g1, band)
    for x in range(n1):
        e1[x] = w1[x] * g1[x]
    smooth(n1, 2, e1, g1, w1)
    restrict(n1, 1, e1, g1, dp1_1, g2)
    for x in range(n2):
        e2[x] = w2[x] * g2[x]
    for _ in range(3):
        smooth(n2, 4, e2, g2, w2)
    for x in range(n1):
        e1[x] = e1[x] + e2[x // 2]
    for _ in range(2):
        smooth(n1, 2, e1, g1, w1)
    for x in range(n0):
        e0[x] = e0[x] + e1[x // 2]
    for _ in range(2):
        smooth0(n0, e0, g0, w0, band)


def send_x(idx, v, out_a, out_b):
    width = out_a.shape[0]
    low, high = 1, BX + 1 - width
    out_a[...] = v[pl.ds(jnp.where(idx[0] == 0, high, low), width)]
    out_b[...] = v[pl.ds(jnp.where(idx[0] == 0, low, high), width)]


def partner_b(idx, in_b):
    return jnp.where((idx[2] + idx[3]) == 0, in_b[idx[0]], 0.0)


def add_x(idx, w, in_a, in_b):
    width = in_a.shape[0]
    low, high = 5 - width, CX + 1
    a = jnp.where(idx[0] == 0, high, low)
    b = jnp.where(idx[0] == 0, low, high)
    w[pl.ds(a, width)] = w[pl.ds(a, width)] + in_a[...]
    w[pl.ds(b, width)] = w[pl.ds(b, width)] + partner_b(idx, in_b)


def pack_x_kernel(idx, r, s, out_a, out_b, sems):
    a = jnp.where(idx[0] == 0, CX - 2, 0)
    b = jnp.where(idx[0] == 0, 0, CX - 2)
    copies = [
        pltpu.make_async_copy(src.at[pl.ds(first, 2)], out.at[k], sems.at[2 * k + n])
        for k, src in enumerate((r, s))
        for n, (first, out) in enumerate(((a, out_a), (b, out_b)))
    ]
    for copy in copies:
        copy.start()
    for copy in copies:
        copy.wait()


def box_kernel(idx, r, s, in_a, in_b, rbox, sbox, out_a, out_b, pack):
    even = idx[0] == 0
    a = jnp.where(even, CX + 2, 0)
    b = jnp.where(even, 0, CX + 2)
    from_b = partner_b(idx, in_b)
    for k, (src, dst) in enumerate(((r, rbox), (s, sbox))):
        dst[...] = jnp.zeros_like(dst)
        for x in range(CX):
            dst[x + 2, 3 : 3 + CY, :] = src[x]
        for x in range(2):
            dst[a + x, 3 : 3 + CY, :] = in_a[k, x]
            dst[b + x, 3 : 3 + CY, :] = from_b[k, x]
        for x in range(BX):
            pack[0, 4 * x + 2 * k : 4 * x + 2 * k + 2, :] = dst[x, 3:5, :]
            pack[1, 4 * x + 2 * k : 4 * x + 2 * k + 2, :] = dst[x, 33:35, :]
    up = jnp.where(idx[1] == 0, 1, 0)
    out_a[...] = pack[up]
    out_b[...] = pack[1 - up]


def first_kernel(
    idx, rin, sin, in_a, in_b,
    r0, v, out_a, out_b, dp1_0, w0, dp1_1, w1, w2,
    got, s0, s1, e1, g1, e2, g2, band,
):
    up = jnp.where(idx[1] == 0, 1, 0)
    got[up] = in_a[...]
    got[1 - up] = jnp.where((idx[4] + idx[5]) == 0, in_b[idx[1]], 0.0)
    row = rows()
    inside = (row >= 1) & (row < 37)
    for k, (src, dst) in enumerate(((rin, r0), (sin, s0))):
        dst[...] = src[...]
        for x in range(BX):
            dst[x, 1:3, :] = got[0, 4 * x + 2 * k : 4 * x + 2 * k + 2, :]
            dst[x, 35:37, :] = got[1, 4 * x + 2 * k : 4 * x + 2 * k + 2, :]

    def coefficients(n, scale, s, dp1, w):
        for x in range(n):
            d = CENTER + scale * s[x]
            if dp1 is not None:
                dp1[x] = d + 1.0
            w[x] = jnp.where(inside, RELAX / d, 0.0)

    coefficients(BX, 1.0, s0, dp1_0, w0)
    for x in range(BX // 2):
        s1[x] = 0.125 * pair_sum(s0[2 * x] + s0[2 * x + 1], 0)
    coefficients(BX // 2, 4.0, s1, dp1_1, w1)
    for x in range(BX // 4):
        s0[x] = 0.125 * pair_sum(s1[2 * x] + s1[2 * x + 1], 1)
    coefficients(BX // 4, 16.0, s0, None, w2)
    band[...] = band_matrix(2, 1)
    v[0] = jnp.zeros((ROWS, CZ), F32)
    v[WX - 1] = jnp.zeros((ROWS, CZ), F32)
    vcycle(v.at[pl.ds(1, BX)], r0, dp1_0, w0, dp1_1, w1, w2, e1, g1, e2, g2, band)
    send_x(idx, v, out_a, out_b)


def pack_y_kernel(idx, v, in_a, in_b, out_a, out_b, w, pack):
    width = in_a.shape[0]
    x0 = 5 - width
    for x in range(WX):
        w[x, 0:8, :] = v[x, 0:8, :]
        w[x, 8:16, :] = v[x, 32:40, :]
    a = jnp.where(idx[0] == 0, CX + 1, x0)
    b = jnp.where(idx[0] == 0, x0, CX + 1)
    from_b = partner_b(idx, in_b)
    for first, src in ((a, in_a), (b, from_b)):
        for x in range(width):
            w[first + x, 0:8, :] = w[first + x, 0:8, :] + src[x, 0:8, :]
            w[first + x, 8:16, :] = w[first + x, 8:16, :] + src[x, 32:40, :]
    pack[:, pack.shape[1] - 8 :, :] = jnp.zeros((2, 8, CZ), F32)
    for x in range(x0, WX - x0):
        at = width * (x - x0)
        pack[0, at : at + width, :] = w[x, 1 : 1 + width, :]
        pack[1, at : at + width, :] = w[x, 13 - width : 13, :]
    up = jnp.where(idx[1] == 0, 1, 0)
    out_a[...] = pack[up]
    out_b[...] = pack[1 - up]


def assemble(idx, w, v, xa, xb, ya, yb, got):
    width = xa.shape[0]
    x0 = 5 - width
    w[...] = v[...]
    add_x(idx, w, xa, xb)
    up = jnp.where(idx[1] == 0, 1, 0)
    got[up] = ya[...]
    got[1 - up] = jnp.where((idx[4] + idx[5]) == 0, yb[idx[1]], 0.0)
    row = rows()
    mask = jnp.where(((row >= 3) | (idx[4] == 0)) & ((row < 3 + CY) | (idx[5] == 0)), 1.0, 0.0)
    for x in range(x0, WX - x0):
        at = width * (x - x0)
        w[x, x0:5, :] = w[x, x0:5, :] + got[0, at : at + width, :]
        w[x, 33 : 33 + width, :] = w[x, 33 : 33 + width, :] + got[1, at : at + width, :]
        m = mask
        if x < 3:
            m = mask * jnp.where(idx[2] == 0, 1.0, 0.0)
        if x >= CX + 3:
            m = mask * jnp.where(idx[3] == 0, 1.0, 0.0)
        w[x] = w[x] * m


def box_mask(idx, x):
    row = rows()
    low = jnp.where(idx[4] == 0, 1, 3)
    high = jnp.where(idx[5] == 0, 37, 35)
    m = jnp.where((row >= low) & (row < high), 1.0, 0.0)
    if x < 2:
        m = m * jnp.where(idx[2] == 0, 1.0, 0.0)
    if x >= CX + 2:
        m = m * jnp.where(idx[3] == 0, 1.0, 0.0)
    return m


def next_kernel(
    idx, vin, xa, xb, ya, yb, rin, dp1_0, w0, dp1_1, w1, w2,
    z, r, v, out_a, out_b,
    w, got, e1, g1, e2, g2, band,
):
    assemble(idx, w, vin, xa, xb, ya, yb, got)
    z[...] = w[pl.ds(3, CX)]

    def emit(x, total):
        if 1 <= x <= BX:
            image = dp1_0[x - 1] * w[x] - total
            r[x - 1] = rin[x - 1] - (STEP * box_mask(idx, x - 1)) * image

    wide_stencil(WX, w, band_matrix(3, 1), emit)
    band[...] = band_matrix(2, 1)
    v[0] = jnp.zeros((ROWS, CZ), F32)
    v[WX - 1] = jnp.zeros((ROWS, CZ), F32)
    vcycle(v.at[pl.ds(1, BX)], r, dp1_0, w0, dp1_1, w1, w2, e1, g1, e2, g2, band)
    send_x(idx, v, out_a, out_b)


def lane_sums(values):
    lane = lax.broadcasted_iota(jnp.int32, (1, CZ), 1)
    out = jnp.zeros((1, CZ), F32)
    for k, s in enumerate(values):
        part = jnp.sum(jnp.sum(s, axis=0, keepdims=True), axis=1, keepdims=True)
        out = out + jnp.where(lane == k, part, 0.0)
    return out


def own_rows():
    row = rows()
    return jnp.where((row >= 3) & (row < 3 + CY), 1.0, 0.0)


def early_kernel(z0, z1, r0, r1, r2, sums):
    own = own_rows()
    acc = [jnp.zeros((ROWS, CZ), F32) for _ in range(5)]
    for x in range(CX):
        a0, a1 = z0[x] * own, z1[x] * own
        b0, b1, b2 = r0[x + 2], r1[x + 2], r2[x + 2]
        terms = (a0 * b0, a0 * b1, a0 * b2, a1 * b1, a1 * b2)
        acc = [s + t for s, t in zip(acc, terms)]
    sums[...] = jnp.broadcast_to(lane_sums([acc[0] * 0.0] * 2 + acc), sums.shape)


def dots_kernel(idx, vin, xa, xb, ya, yb, dp1_0, r2, early, z2, u2, sums, w, got):
    assemble(idx, w, vin, xa, xb, ya, yb, got)
    own = own_rows()
    acc = [jnp.zeros((ROWS, CZ), F32) for _ in range(2)]

    def emit(x, total):
        if 3 <= x < 3 + CX:
            here = w[x]
            image = dp1_0[x - 1] * here - total
            z2[x - 3] = here
            u2[x - 3] = image
            here = here * own
            acc[0] = acc[0] + here * r2[x - 1]
            acc[1] = acc[1] + here * image

    wide_stencil(WX, w, band_matrix(3, 1), emit)
    sums[...] = jnp.broadcast_to(early[0:1, :] + lane_sums(acc), sums.shape)


def final_kernel(gathered, z0, z1, z2, r0, r1, r2, u2, x_out, r_out):
    row = jnp.sum(gathered[...], axis=0, keepdims=True)
    lane = lax.broadcasted_iota(jnp.int32, (1, CZ), 1)
    m22, h22, m00, m01, m02, m11, m12 = (
        jnp.sum(jnp.where(lane == k, row, 0.0), axis=1, keepdims=True) for k in range(7)
    )
    inv = 1.0 / STEP
    h00, h01, h02 = inv * (m00 - m01), inv * (m01 - m02), inv * (m02 - m12)
    h11, h12 = inv * (m11 - m12), inv * (m12 - m22)
    l10, l20 = h01 / h00, h02 / h00
    d1 = h11 - l10 * h01
    q = h12 - l10 * h02
    l21 = q / d1
    d2 = h22 - l20 * h02 - l21 * q
    y1 = m01 - l10 * m00
    y2 = m02 - l20 * m00 - l21 * y1
    c2 = y2 / d2
    c1 = y1 / d1 - l21 * c2
    c0 = m00 / h00 - l10 * c1 - l20 * c2
    f0, f1 = inv * c0, inv * c1
    for x in range(CX):
        xs = c0 * z0[x] + c1 * z1[x] + c2 * z2[x]
        b0, b1 = r0[x + 2], r1[x + 2]
        rs = b0 - f0 * (b0 - b1) - f1 * (b1 - r2[x + 2]) - c2 * u2[x]
        x_out[x] = xs[3 : 3 + CY, :]
        r_out[x] = rs[3 : 3 + CY, :]


def vmem(n):
    return [pl.BlockSpec(memory_space=pltpu.VMEM) for _ in range(n)]


def call(body, n_in, outs, scratch=(), smem=True, space=pltpu.VMEM):
    in_specs = [pl.BlockSpec(memory_space=space) for _ in range(n_in)]
    kernel = body
    if smem:

        def kernel(*refs):
            body(place(), *refs)

    return pl.pallas_call(
        kernel,
        out_shape=outs,
        in_specs=in_specs,
        out_specs=vmem(len(outs)),
        scratch_shapes=[pltpu.VMEM(s, F32) if isinstance(s, tuple) else s for s in scratch],
        interpret=INTERPRET,
        compiler_params=pltpu.CompilerParams(vmem_limit_bytes=VMEM_LIMIT),
    )


INTERPRET = False
VMEM_LIMIT = 16 * 2**20


def pairs(n_gx, n_gy, axis, odd):
    count = n_gx if axis == 0 else n_gy
    result = []
    for i in range(n_gx):
        for j in range(n_gy):
            here = i if axis == 0 else j
            there = ((here + odd) ^ 1) - odd
            if 0 <= there < count:
                target = (there, j) if axis == 0 else (i, there)
                result.append((i * n_gy + j, target[0] * n_gy + target[1]))
    return result


def solution(mesh):
    n_gx, n_gy = mesh.shape["gx"], mesh.shape["gy"]

    far = [[i * n_gy + j, i * n_gy + j + 1] for i in range(n_gx) for j in range(1, n_gy - 1, 2)]
    far += [[i * n_gy + j, (i + 1) * n_gy + j] for i in range(0, n_gx, 2) for j in (0, n_gy - 1)]
    neighbours = [[i * n_gy + j, (i + 1) * n_gy + j] for i in range(1, n_gx - 1, 2) for j in range(n_gy)]
    neighbours += [[i * n_gy + j, i * n_gy + j + 1] for i in (0, n_gx - 1) for j in range(0, n_gy, 2)]

    def swap_x(a, b):
        return (
            lax.ppermute(a, AX, pairs(n_gx, n_gy, 0, 0)),
            lax.all_gather(b, AX, axis_index_groups=neighbours),
        )

    def swap_y(a, b):
        a = lax.ppermute(a, AX, pairs(n_gx, n_gy, 1, 0))
        b = lax.all_gather(b, AX, axis_index_groups=far)
        return a, b

    box = sds(BX, ROWS, CZ)
    half = sds(BX // 2, ROWS, CZ)
    quarter = sds(BX // 4, ROWS, CZ)
    wide = sds(WX, ROWS, CZ)
    own = sds(CX, ROWS, CZ)
    band = pltpu.VMEM((2 * CZ, CZ), jnp.bfloat16)
    coarse = [half.shape, half.shape, quarter.shape, quarter.shape, band]

    def yrows(width):
        return -(-(CX - 4 + 2 * width) * width // 8) * 8

    def on_device(right_side, shift):
        def exchange(v, xa, xb):
            width = xa.shape[0]
            xa, xb = swap_x(xa, xb)
            size = yrows(width)
            ya, yb = call(
                pack_y_kernel, 3, [sds(size, CZ)] * 2, [(WX, 16, CZ), (2, size, CZ)]
            )(v, xa, xb)
            return (v, xa, xb) + swap_y(ya, yb)

        first = sds(2, 2, CY, CZ)
        xa, xb = call(
            pack_x_kernel, 2, [first, first], [pltpu.SemaphoreType.DMA((4,))], space=pltpu.HBM
        )(*(pltpu.with_memory_space_constraint(a, pltpu.HBM) for a in (right_side, shift)))
        xa, xb = swap_x(xa, xb)
        strip = sds(IROWS, CZ)
        rbox, sbox, ya, yb = call(
            box_kernel, 4, [box, box, strip, strip], [(2, IROWS, CZ)]
        )(right_side, shift, xa, xb)
        ya, yb = swap_y(ya, yb)
        r0, v, xa, xb, *coefs = call(
            first_kernel,
            4,
            [box, wide, sds(5, ROWS, CZ), sds(5, ROWS, CZ), box, box, half, half, quarter],
            [(2, IROWS, CZ), box.shape, half.shape] + coarse,
        )(rbox, sbox, ya, yb)
        residuals, images = [r0], []
        for width in (5, 3):
            z, r, v, xa, xb = call(
                next_kernel,
                11,
                [own, box, wide, sds(width, ROWS, CZ), sds(width, ROWS, CZ)],
                [wide.shape, (2, yrows(5), CZ)] + coarse,
            )(*exchange(v, xa, xb), residuals[-1], *coefs)
            images.append(z)
            residuals.append(r)
        early = call(early_kernel, 5, [sds(8, CZ)], smem=False)(*images, *residuals)[0]
        z2, u2, sums = call(
            dots_kernel, 8, [own, own, sds(n_gx * n_gy, CZ)], [wide.shape, (2, yrows(3), CZ)]
        )(*exchange(v, xa, xb), coefs[0], residuals[-1], early)
        gathered = lax.all_to_all(sums, AX, 0, 0, tiled=True)
        x, r = call(
            final_kernel, 8, [sds(CX, CY, CZ), sds(CX, CY, CZ)], smem=False
        )(gathered, *images, z2, *residuals, u2)
        return x, r

    spec = P("gx", "gy", None)
    return jax.shard_map(
        on_device, mesh=mesh, in_specs=(spec, spec), out_specs=(spec, spec), check_vma=False
    )
```

profile of v0, /device:TPU:1, one launch (start us, length us, event | category | flops | bytes accessed | tf_op | source)
XLA Modules:
  0.0 92.3 jit_solution(1409302862867387482)
XLA Ops:
  0.6 0.9 shard_map.41
  1.6 1.5 %collective-permute-start = (f32[2,2,32,128]{3,2,1,0:T(8,128)S(1)}, f32[2,2,32,128]{3,2,1,0:T(8,128)S(1)}, u32[]{:S(2)}, u32[]{:S(2)}) collective-permute-start(f32[2,2,32,128]{3,2,1,0:T(8,128)S(1)} %get-tuple-element.36), channel_id=1, source_target_pairs={{0,8},{1,9},{2,10},{3,11},{4,12},{5,13},{6,14},{7,15},{8,0},{9,1},... | collective-permute-start | bytes 196616 | tf_op jit(solution)/shard_map/ppermute | solution.py:452
  3.0 4.7 %all-gather = f32[4,2,32,128]{3,2,1,0:T(8,128)S(1)} all-gather(f32[2,2,32,128]{3,2,1,0:T(8,128)S(1)} %get-tuple-element.37), channel_id=2, replica_groups={{8,16},{9,17},{10,18},{11,19},{12,20},{13,21},{14,22},{15,23},{24,32},{..., dimensions={0}, use_global_device_ids=true | all-gather | bytes 196608 | tf_op jit(solution)/shard_map/all_gather | solution.py:453
  7.8 2.6 %collective-permute-start.1 = (f32[80,128]{1,0:T(8,128)S(1)}, f32[80,128]{1,0:T(8,128)S(1)}, u32[]{:S(2)}, u32[]{:S(2)}) collective-permute-start(f32[80,128]{1,0:T(8,128)S(1)} %get-tuple-element.40), channel_id=1, source_target_pairs={{0,1},{1,0},{2,3},{3,2},{4,5},{5,4},{6,7},{7,6},{8,9},{9,8},{10,11... | collective-permute-start | bytes 122888 | tf_op jit(solution)/shard_map/ppermute | solution.py:457
  10.5 3.9 %all-gather.1 = f32[160,128]{1,0:T(8,128)S(1)} all-gather(f32[80,128]{1,0:T(8,128)S(1)} %get-tuple-element.41), channel_id=3, replica_groups={{1,2},{3,4},{5,6},{9,10},{11,12},{13,14},{17,18},{19,20},{21,22},{25,26..., dimensions={0}, use_global_device_ids=true | all-gather | bytes 122880 | tf_op jit(solution)/shard_map/all_gather | solution.py:458
  14.4 2.5 %shard_map.43 = (f32[20,40,128]{2,1,0:T(8,128)S(1)}, f32[22,40,128]{2,1,0:T(8,128)S(1)}, f32[5,40,128]{2,1,0:T(8,128)S(1)}, f32[5,40,128]{2,1,0:T(8,128)S(1)}, f...) custom-call(f32[20,40,128]{2,1,0:T(8,128)S(1)} %get-tuple-element.38, ...), custom_call_target="tpu_custom_call" | custom-call | tf_op jit(solution)/shard_map/pallas_call | solution.py:492
  16.8 0.9 %collective-permute-start.2 = (f32[5,40,128]{2,1,0:T(8,128)S(1)}, f32[5,40,128]{2,1,0:T(8,128)S(1)}, u32[]{:S(2)}, u32[]{:S(2)}) collective-permute-start(f32[5,40,128]{2,1,0:T(8,128)S(1)} %get-tuple-element.43), channel_id=1, source_target_pairs={{0,8},{1,9},{2,10},{3,11},{4,12},{5,13},{6,14},{7,15},{8,0},{9,1},... | collective-permute-start | bytes 307208 | tf_op jit(solution)/shard_map/ppermute | solution.py:452
  17.8 4.8 %all-gather.2 = f32[10,40,128]{2,1,0:T(8,128)S(1)} all-gather(f32[5,40,128]{2,1,0:T(8,128)S(1)} %get-tuple-element.44), channel_id=4, replica_groups={{8,16},{9,17},{10,18},{11,19},{12,20},{13,21},{14,22},{15,23},{24,32},{..., dimensions={0}, use_global_device_ids=true | all-gather | bytes 307200 | tf_op jit(solution)/shard_map/all_gather | solution.py:453
  22.6 5.2 %collective-permute-start.3 = (f32[112,128]{1,0:T(8,128)S(1)}, f32[112,128]{1,0:T(8,128)S(1)}, u32[]{:S(2)}, u32[]{:S(2)}) collective-permute-start(f32[112,128]{1,0:T(8,128)S(1)} %get-tuple-element.45), channel_id=1, source_target_pairs={{0,1},{1,0},{2,3},{3,2},{4,5},{5,4},{6,7},{7,6},{8,9},{9,8},{10,11... | collective-permute-start | bytes 172040 | tf_op jit(solution)/shard_map/ppermute | solution.py:457
  27.8 3.6 %all-gather.3 = f32[224,128]{1,0:T(8,128)S(1)} all-gather(f32[112,128]{1,0:T(8,128)S(1)} %get-tuple-element.46), channel_id=5, replica_groups={{1,2},{3,4},{5,6},{9,10},{11,12},{13,14},{17,18},{19,20},{21,22},{25,26..., dimensions={0}, use_global_device_ids=true | all-gather | bytes 172032 | tf_op jit(solution)/shard_map/all_gather | solution.py:458
  31.4 2.8 %shard_map.45 = (f32[16,40,128]{2,1,0:T(8,128)S(1)}, f32[20,40,128]{2,1,0:T(8,128)S(1)}, f32[22,40,128]{2,1,0:T(8,128)S(1)}, f32[5,40,128]{2,1,0:T(8,128)S(1)}, f32[5,40,128]{2,1,0:T(8,128)S(1)}) custom-call(f32[22,40,128]{2,1,0:T(8,128)S(1)} %get-tuple-element.42.refs_0_, f32[5,40,128]{2,1,0:T(8,128)S(1)} %collective-permute-done.2.refs_1_, ...), custom_call_target="tpu_custom_call" | custom-call | tf_op jit(solution)/shard_map/pallas_call | solution.py:500
  34.2 0.7 collective-permute-start.4
  34.9 4.8 %all-gather.4 = f32[10,40,128]{2,1,0:T(8,128)S(1)} all-gather(f32[5,40,128]{2,1,0:T(8,128)S(1)} %get-tuple-element.55), channel_id=6, replica_groups={{8,16},{9,17},{10,18},{11,19},{12,20},{13,21},{14,22},{15,23},{24,32},{..., dimensions={0}, use_global_device_ids=true | all-gather | bytes 307200 | tf_op jit(solution)/shard_map/all_gather | solution.py:453
  39.8 5.4 %collective-permute-start.5 = (f32[112,128]{1,0:T(8,128)S(1)}, f32[112,128]{1,0:T(8,128)S(1)}, u32[]{:S(2)}, u32[]{:S(2)}) collective-permute-start(f32[112,128]{1,0:T(8,128)S(1)} %get-tuple-element.56), channel_id=1, source_target_pairs={{0,1},{1,0},{2,3},{3,2},{4,5},{5,4},{6,7},{7,6},{8,9},{9,8},{10,11... | collective-permute-start | bytes 172040 | tf_op jit(solution)/shard_map/ppermute | solution.py:457
  45.1 3.6 %all-gather.5 = f32[224,128]{1,0:T(8,128)S(1)} all-gather(f32[112,128]{1,0:T(8,128)S(1)} %get-tuple-element.57), channel_id=7, replica_groups={{1,2},{3,4},{5,6},{9,10},{11,12},{13,14},{17,18},{19,20},{21,22},{25,26..., dimensions={0}, use_global_device_ids=true | all-gather | bytes 172032 | tf_op jit(solution)/shard_map/all_gather | solution.py:458
  48.7 2.8 %shard_map.47 = (f32[16,40,128]{2,1,0:T(8,128)S(1)}, f32[20,40,128]{2,1,0:T(8,128)S(1)}, f32[22,40,128]{2,1,0:T(8,128)S(1)}, f32[3,40,128]{2,1,0:T(8,128)S(1)}, f32[3,40,128]{2,1,0:T(8,128)S(1)}) custom-call(f32[22,40,128]{2,1,0:T(8,128)S(1)} %get-tuple-element.53.refs_0_, f32[5,40,128]{2,1,0:T(8,128)S(1)} %collective-permute-done.4.refs_1_, ...), custom_call_target="tpu_custom_call" | custom-call | tf_op jit(solution)/shard_map/pallas_call | solution.py:500
  51.6 0.7 collective-permute-start.6
  52.3 4.3 %all-gather.6 = f32[6,40,128]{2,1,0:T(8,128)S(1)} all-gather(f32[3,40,128]{2,1,0:T(8,128)S(1)} %get-tuple-element.61), channel_id=8, replica_groups={{8,16},{9,17},{10,18},{11,19},{12,20},{13,21},{14,22},{15,23},{24,32},{..., dimensions={0}, use_global_device_ids=true | all-gather | bytes 184320 | tf_op jit(solution)/shard_map/all_gather | solution.py:453
  56.7 7.9 %collective-permute-start.7 = (f32[56,128]{1,0:T(8,128)S(1)}, f32[56,128]{1,0:T(8,128)S(1)}, u32[]{:S(2)}, u32[]{:S(2)}) collective-permute-start(f32[56,128]{1,0:T(8,128)S(1)} %get-tuple-element.62), channel_id=1, source_target_pairs={{0,1},{1,0},{2,3},{3,2},{4,5},{5,4},{6,7},{7,6},{8,9},{9,8},{10,11... | collective-permute-start | bytes 86024 | tf_op jit(solution)/shard_map/ppermute | solution.py:457
  64.6 0.2 shard_map.49.refs_7_
  64.8 3.9 %all-gather.7 = f32[112,128]{1,0:T(8,128)S(1)} all-gather(f32[56,128]{1,0:T(8,128)S(1)} %get-tuple-element.63), channel_id=9, replica_groups={{1,2},{3,4},{5,6},{9,10},{11,12},{13,14},{17,18},{19,20},{21,22},{25,26..., dimensions={0}, use_global_device_ids=true | all-gather | bytes 86016 | tf_op jit(solution)/shard_map/all_gather | solution.py:458
  68.6 0.6 shard_map.50
  69.2 22.0 %all_to_all.11 = f32[128,1,128]{2,1,0:T(1,128)S(1)} all-to-all(f32[128,1,128]{2,1,0:T(1,128)S(1)} %bitcast.24), channel_id=1, replica_groups=mesh['gx'=16,'gy'=8] {'gx','gy'}, dimensions={0} | all-to-all | bytes 131072 | tf_op jit(solution)/shard_map/all_to_all | solution.py:512
  91.2 1.1 %shard_map.51 = (f32[16,32,128]{2,1,0:T(8,128)}, f32[16,32,128]{2,1,0:T(8,128)}) custom-call(f32[128,128]{1,0:T(8,128)S(1)} %bitcast.22, f32[16,40,128]{2,1,0:T(8,128)S(1)} %get-tuple-element.65.z0, f32[16,40,128]{2,1,0:T(8,128)S(1)} %get-tuple-element.66.z1, f32[16,40,128]{2,1,0:T(8,128)S(1)} %get-tuple-element.68.z2, ...), custom_call_target="tpu_custom_call" | custom-call | tf_op jit(solution)/shard_map/pallas_call | solution.py:513
  (16 shorter events, 0.3 us)
Async XLA Ops:
  0.6 7.1 %copy-start.1 = (f32[16,32,128]{2,1,0:T(8,128)S(1)}, f32[16,32,128]{2,1,0:T(8,128)}, u32[]{:S(2)}) copy-start(f32[16,32,128]{2,1,0:T(8,128)} %refs_1_.3) | copy-start | bytes 786436
  0.6 7.0 %copy-start = (f32[16,32,128]{2,1,0:T(8,128)S(1)}, f32[16,32,128]{2,1,0:T(8,128)}, u32[]{:S(2)}) copy-start(f32[16,32,128]{2,1,0:T(8,128)} %refs_0_.3) | copy-start | bytes 786436
  1.6 6.1 %collective-permute-start = (f32[2,2,32,128]{3,2,1,0:T(8,128)S(1)}, f32[2,2,32,128]{3,2,1,0:T(8,128)S(1)}, u32[]{:S(2)}, u32[]{:S(2)}) collective-permute-start(f32[2,2,32,128]{3,2,1,0:T(8,128)S(1)} %get-tuple-element.36), channel_id=1, source_target_pairs={{0,8},{1,9},{2,10},{3,11},{4,12},{5,13},{6,14},{7,15},{8,0},{9,1},... | collective-permute-start | bytes 196616 | tf_op jit(solution)/shard_map/ppermute | solution.py:452
  7.8 6.5 %collective-permute-start.1 = (f32[80,128]{1,0:T(8,128)S(1)}, f32[80,128]{1,0:T(8,128)S(1)}, u32[]{:S(2)}, u32[]{:S(2)}) collective-permute-start(f32[80,128]{1,0:T(8,128)S(1)} %get-tuple-element.40), channel_id=1, source_target_pairs={{0,1},{1,0},{2,3},{3,2},{4,5},{5,4},{6,7},{7,6},{8,9},{9,8},{10,11... | collective-permute-start | bytes 122888 | tf_op jit(solution)/shard_map/ppermute | solution.py:457
  16.8 5.7 %collective-permute-start.2 = (f32[5,40,128]{2,1,0:T(8,128)S(1)}, f32[5,40,128]{2,1,0:T(8,128)S(1)}, u32[]{:S(2)}, u32[]{:S(2)}) collective-permute-start(f32[5,40,128]{2,1,0:T(8,128)S(1)} %get-tuple-element.43), channel_id=1, source_target_pairs={{0,8},{1,9},{2,10},{3,11},{4,12},{5,13},{6,14},{7,15},{8,0},{9,1},... | collective-permute-start | bytes 307208 | tf_op jit(solution)/shard_map/ppermute | solution.py:452
  22.6 8.8 %collective-permute-start.3 = (f32[112,128]{1,0:T(8,128)S(1)}, f32[112,128]{1,0:T(8,128)S(1)}, u32[]{:S(2)}, u32[]{:S(2)}) collective-permute-start(f32[112,128]{1,0:T(8,128)S(1)} %get-tuple-element.45), channel_id=1, source_target_pairs={{0,1},{1,0},{2,3},{3,2},{4,5},{5,4},{6,7},{7,6},{8,9},{9,8},{10,11... | collective-permute-start | bytes 172040 | tf_op jit(solution)/shard_map/ppermute | solution.py:457
  34.2 5.5 %collective-permute-start.4 = (f32[5,40,128]{2,1,0:T(8,128)S(1)}, f32[5,40,128]{2,1,0:T(8,128)S(1)}, u32[]{:S(2)}, u32[]{:S(2)}) collective-permute-start(f32[5,40,128]{2,1,0:T(8,128)S(1)} %get-tuple-element.54), channel_id=1, source_target_pairs={{0,8},{1,9},{2,10},{3,11},{4,12},{5,13},{6,14},{7,15},{8,0},{9,1},... | collective-permute-start | bytes 307208 | tf_op jit(solution)/shard_map/ppermute | solution.py:452
  39.8 9.0 %collective-permute-start.5 = (f32[112,128]{1,0:T(8,128)S(1)}, f32[112,128]{1,0:T(8,128)S(1)}, u32[]{:S(2)}, u32[]{:S(2)}) collective-permute-start(f32[112,128]{1,0:T(8,128)S(1)} %get-tuple-element.56), channel_id=1, source_target_pairs={{0,1},{1,0},{2,3},{3,2},{4,5},{5,4},{6,7},{7,6},{8,9},{9,8},{10,11... | collective-permute-start | bytes 172040 | tf_op jit(solution)/shard_map/ppermute | solution.py:457
  51.6 5.0 %collective-permute-start.6 = (f32[3,40,128]{2,1,0:T(8,128)S(1)}, f32[3,40,128]{2,1,0:T(8,128)S(1)}, u32[]{:S(2)}, u32[]{:S(2)}) collective-permute-start(f32[3,40,128]{2,1,0:T(8,128)S(1)} %get-tuple-element.60), channel_id=1, source_target_pairs={{0,8},{1,9},{2,10},{3,11},{4,12},{5,13},{6,14},{7,15},{8,0},{9,1},... | collective-permute-start | bytes 184328 | tf_op jit(solution)/shard_map/ppermute | solution.py:452
  56.7 12.0 %collective-permute-start.7 = (f32[56,128]{1,0:T(8,128)S(1)}, f32[56,128]{1,0:T(8,128)S(1)}, u32[]{:S(2)}, u32[]{:S(2)}) collective-permute-start(f32[56,128]{1,0:T(8,128)S(1)} %get-tuple-element.62), channel_id=1, source_target_pairs={{0,1},{1,0},{2,3},{3,2},{4,5},{5,4},{6,7},{7,6},{8,9},{9,8},{10,11... | collective-permute-start | bytes 86024 | tf_op jit(solution)/shard_map/ppermute | solution.py:457
where the time goes:
time: 92.5 us; the launch traced here: 92.3 us
  blocking collectives  55.4 us (60%)
  starting transfers between devices  25 us (27%)
  Pallas kernels  11.2 us (12%)
    all_to_all x1, blocking collectives, on_device(): gathered = lax.all_to_all(sums, AX, 0, 0, tiled=True)  22 us
    ppermute x4, starting transfers between devices, swap_y(): a = lax.ppermute(a, AX, pairs(n_gx, n_gy, 1, 0))  21.1 us
    all_gather x4, blocking collectives, swap_x(): lax.all_gather(b, AX, axis_index_groups=neighbours)  18.5 us
    all_gather x4, blocking collectives, swap_y(): b = lax.all_gather(b, AX, axis_index_groups=far)  14.9 us
    pallas_call x2, Pallas kernels, on_device(): call(next_kernel, 11, [own, box, wide, sds(width, ROWS, CZ), sds(width, R...  5.66 us
    ppermute x4, starting transfers between devices, swap_x(): lax.ppermute(a, AX, pairs(n_gx, n_gy, 0, 0))  3.84 us
    pallas_call x1, Pallas kernels, on_device(): call(first_kernel, 4, [box, wide, sds(5, ROWS, CZ), sds(5, ROWS, CZ), box...  2.47 us
  transfers between devices with their start and end apart: 8, of which 0 were waited for; matrix products, arithmetic and copies ran while one was open for 0% of the time, Pallas kernels for 0%

commit v1 on v0

--- a/solution.py
+++ b/solution.py
@@ -1,5 +1,6 @@
 import jax
 import jax.numpy as jnp
+import numpy as np
 from jax import lax
 from jax.experimental import pallas as pl
 from jax.experimental.pallas import tpu as pltpu
@@ -12,6 +13,7 @@
 AX = ("gx", "gy")
 CX, CY, CZ = 16, 32, 128
 ROWS = 40
+CROWS = 24
 BX = CX + 4
 WX = CX + 6
 F32 = jnp.float32
@@ -28,25 +30,13 @@
     return jax.ShapeDtypeStruct(shape, F32)
 
 
-def lanes():
-    return lax.broadcasted_iota(jnp.int32, (ROWS, CZ), 1)
-
-
 def rows():
     return lax.broadcasted_iota(jnp.int32, (ROWS, CZ), 0)
 
 
-def zy_sum(p, sh):
-    lane = lanes()
-    zs = p + jnp.where(lane >= sh, pltpu.roll(p, sh, 1), 0.0)
-    zs = zs + jnp.where(lane < CZ - sh, pltpu.roll(p, CZ - sh, 1), 0.0)
-    return zs + pltpu.roll(zs, sh, 0) + pltpu.roll(zs, ROWS - sh, 0)
-
-
-def band_matrix(terms, sh):
-    at = lax.broadcasted_iota(jnp.int32, (terms * CZ, CZ), 0) & (CZ - 1)
-    gap = jnp.abs(at - lax.broadcasted_iota(jnp.int32, (terms * CZ, CZ), 1))
-    return jnp.where((gap == 0) | (gap == sh), 1.0, 0.0).astype(jnp.bfloat16)
+def lane_matrix():
+    gap = np.abs(np.arange(CZ)[:, None] - np.arange(CZ)[None, :])
+    return np.tile(gap <= 1, (3, 1)).astype(jnp.bfloat16)
 
 
 def z_sums(planes, band):
@@ -61,64 +51,68 @@
     return sums.reshape(n, ROWS, CZ)
 
 
-def wide_stencil(n, e, band, emit):
+def x_sums(n, plane, emit):
+    planes = [plane(0)]
+    pair = None
+    for x in range(n):
+        if x + 1 < n:
+            planes.append(plane(x + 1))
+        if x % 2 == 0:
+            pair = planes[x] + planes[x + 1] if x + 1 < n else planes[x]
+            total = pair + planes[x - 1] if x > 0 else pair
+        else:
+            total = pair + planes[x + 1] if x + 1 < n else pair
+        emit(x, total)
+
+
+def stencil(n, e, band, emit):
     sums = z_sums(e[...], band)
 
-    def y_sum(x):
+    def plane(x):
         zs = sums[x]
         return zs + pltpu.roll(zs, 1, 0) + pltpu.roll(zs, ROWS - 1, 0)
 
-    prev, cur = None, y_sum(0)
-    for x in range(n):
-        nxt = y_sum(x + 1) if x + 1 < n else None
-        total = cur
-        if prev is not None:
-            total = total + prev
-        if nxt is not None:
-            total = total + nxt
-        emit(x, total)
-        prev, cur = cur, nxt
-
-
-def stencil(n, sh, load, emit):
-    prev = None
-    cur = zy_sum(load(0), sh)
-    for x in range(n):
-        nxt = zy_sum(load(x + 1), sh) if x + 1 < n else None
-        total = cur
-        if prev is not None:
-            total = total + prev
-        if nxt is not None:
-            total = total + nxt
-        emit(x, total)
-        prev, cur = cur, nxt
-
-
-def pair_sum(a, level):
+    x_sums(n, plane, emit)
+
+
+def coarse_stencil(n, level, e, emit):
+    sy, sz = 2 ** (level - 1), 2**level
+    lane = lax.broadcasted_iota(jnp.int32, (CROWS, CZ), 1)
+
+    def plane(x):
+        p = e[x]
+        zs = p + jnp.where(lane >= sz, pltpu.roll(p, sz, 1), 0.0)
+        zs = zs + jnp.where(lane < CZ - sz, pltpu.roll(p, CZ - sz, 1), 0.0)
+        return zs + pltpu.roll(zs, sy, 0) + pltpu.roll(zs, CROWS - sy, 0)
+
+    x_sums(n, plane, emit)
+
+
+def z_pairs(a, level):
     sh = 2**level
-    bit = ((rows() + 7) >> level) & 1
-    a = a + jnp.where(bit == 0, pltpu.roll(a, ROWS - sh, 0), pltpu.roll(a, sh, 0))
-    bit = (lanes() >> level) & 1
+    bit = (lax.broadcasted_iota(jnp.int32, a.shape, 1) >> level) & 1
     return a + jnp.where(bit == 0, pltpu.roll(a, CZ - sh, 1), pltpu.roll(a, sh, 1))
 
 
-def smooth0(n, e, g, w, band):
+def blocks1(tmp, x):
+    a = tmp[x, pl.ds(1, CROWS, stride=2), :] + tmp[x, pl.ds(2, CROWS, stride=2), :]
+    return z_pairs(a, 0)
+
+
+def blocks2(a):
+    bit = lax.broadcasted_iota(jnp.int32, (CROWS, CZ), 0) & 1
+    a = a + jnp.where(bit == 0, pltpu.roll(a, CROWS - 1, 0), pltpu.roll(a, 1, 0))
+    return z_pairs(a, 1)
+
+
+def relaxed(e, g, w):
     def emit(x, total):
-        here = e[x]
-        e[x] = (1.0 - RELAX) * here + w[x] * (g[x] + (total - here))
-
-    wide_stencil(n, e, band, emit)
-
-
-def smooth(n, sh, e, g, w):
-    def emit(x, total):
-        here = e[x]
-        e[x] = (1.0 - RELAX) * here + w[x] * (g[x] + (total - here))
-
-    stencil(n, sh, lambda x: e[x], emit)
-
-
-def restrict(n, level, e, g, dp1, g_next, band=None):
+        e[x] = w[1, x] * e[x] + w[0, x] * (g[x] + total)
+
+    return emit
+
+
+def pairwise(e, g, dp1, use):
     held = []
 
     def emit(x, total):
@@ -126,36 +120,51 @@
         if x % 2 == 0:
             held.append(left)
         else:
-            g_next[x // 2] = 0.5 * pair_sum(held.pop() + left, level)
-
-    if band is None:
-        stencil(n, 2**level, lambda x: e[x], emit)
-    else:
-        wide_stencil(n, e, band, emit)
-
-
-def vcycle(e0, g0, dp1_0, w0, dp1_1, w1, w2, e1, g1, e2, g2, band):
+            use(x // 2, held.pop() + left)
+
+    return emit
+
+
+def vcycle(e0, g0, dp1_0, w0, dp1_1, w1, w2, e1, g1, e2, g2, tmp, band):
     n0, n1, n2 = BX, BX // 2, BX // 4
     for x in range(n0):
-        e0[x] = w0[x] * g0[x]
-    smooth0(n0, e0, g0, w0, band)
-    restrict(n0, 0, e0, g0, dp1_0, g1, band)
+        e0[x] = w0[0, x] * g0[x]
+    stencil(n0, e0, band, relaxed(e0, g0, w0))
+
+    def to_level1(k, left):
+        tmp[k, 0:ROWS, :] = left
+        g1[k] = 0.5 * blocks1(tmp, k)
+
+    stencil(n0, e0, band, pairwise(e0, g0, dp1_0, to_level1))
     for x in range(n1):
-        e1[x] = w1[x] * g1[x]
-    smooth(n1, 2, e1, g1, w1)
-    restrict(n1, 1, e1, g1, dp1_1, g2)
+        e1[x] = w1[0, x] * g1[x]
+    coarse_stencil(n1, 1, e1, relaxed(e1, g1, w1))
+
+    def to_level2(k, left):
+        g2[k] = 0.5 * blocks2(left)
+
+    coarse_stencil(n1, 1, e1, pairwise(e1, g1, dp1_1, to_level2))
     for x in range(n2):
-        e2[x] = w2[x] * g2[x]
+        e2[x] = w2[0, x] * g2[x]
     for _ in range(3):
-        smooth(n2, 4, e2, g2, w2)
+        coarse_stencil(n2, 2, e2, relaxed(e2, g2, w2))
     for x in range(n1):
         e1[x] = e1[x] + e2[x // 2]
     for _ in range(2):
-        smooth(n1, 2, e1, g1, w1)
+        coarse_stencil(n1, 1, e1, relaxed(e1, g1, w1))
+    for x in range(n1):
+        tmp[x, pl.ds(1, CROWS, stride=2), :] = e1[x]
+        tmp[x, pl.ds(2, CROWS, stride=2), :] = e1[x]
+        tmp[x, 0:1, :] = jnp.zeros((1, CZ), F32)
     for x in range(n0):
-        e0[x] = e0[x] + e1[x // 2]
+        e0[x] = e0[x] + tmp[x // 2, 0:ROWS, :]
     for _ in range(2):
-        smooth0(n0, e0, g0, w0, band)
+        stencil(n0, e0, band, relaxed(e0, g0, w0))
+
+
+def clear_ends(tmp):
+    for x in range(BX // 2):
+        tmp[x, ROWS:, :] = jnp.zeros((16, CZ), F32)
 
 
 def send_x(idx, v, out_a, out_b):
@@ -213,39 +222,41 @@
 
 
 def first_kernel(
-    idx, rin, sin, in_a, in_b,
+    idx, rin, sin, in_a, in_b, band,
     r0, v, out_a, out_b, dp1_0, w0, dp1_1, w1, w2,
-    got, s0, s1, e1, g1, e2, g2, band,
+    got, s0, s1, e1, g1, e2, g2, tmp,
 ):
     up = jnp.where(idx[1] == 0, 1, 0)
     got[up] = in_a[...]
     got[1 - up] = jnp.where((idx[4] + idx[5]) == 0, in_b[idx[1]], 0.0)
-    row = rows()
-    inside = (row >= 1) & (row < 37)
     for k, (src, dst) in enumerate(((rin, r0), (sin, s0))):
         dst[...] = src[...]
         for x in range(BX):
             dst[x, 1:3, :] = got[0, 4 * x + 2 * k : 4 * x + 2 * k + 2, :]
             dst[x, 35:37, :] = got[1, 4 * x + 2 * k : 4 * x + 2 * k + 2, :]
 
-    def coefficients(n, scale, s, dp1, w):
-        for x in range(n):
-            d = CENTER + scale * s[x]
-            if dp1 is not None:
-                dp1[x] = d + 1.0
-            w[x] = jnp.where(inside, RELAX / d, 0.0)
-
-    coefficients(BX, 1.0, s0, dp1_0, w0)
+    def coefficients(x, scale, s, inside, dp1, w):
+        d = CENTER + scale * s
+        if dp1 is not None:
+            dp1[x] = d + 1.0
+        ratio = RELAX / d
+        w[0, x] = jnp.where(inside, ratio, 0.0)
+        w[1, x] = jnp.where(inside, (1.0 - RELAX) - ratio, 0.0)
+
+    clear_ends(tmp)
+    row = rows()
+    for x in range(BX):
+        coefficients(x, 1.0, s0[x], (row >= 1) & (row < 37), dp1_0, w0)
+    inside = lax.broadcasted_iota(jnp.int32, (CROWS, CZ), 0) < (CY + 4) // 2
     for x in range(BX // 2):
-        s1[x] = 0.125 * pair_sum(s0[2 * x] + s0[2 * x + 1], 0)
-    coefficients(BX // 2, 4.0, s1, dp1_1, w1)
+        tmp[x, 0:ROWS, :] = s0[2 * x] + s0[2 * x + 1]
+        s1[x] = 0.125 * blocks1(tmp, x)
+        coefficients(x, 4.0, s1[x], inside, dp1_1, w1)
     for x in range(BX // 4):
-        s0[x] = 0.125 * pair_sum(s1[2 * x] + s1[2 * x + 1], 1)
-    coefficients(BX // 4, 16.0, s0, None, w2)
-    band[...] = band_matrix(2, 1)
+        coefficients(x, 16.0, 0.125 * blocks2(s1[2 * x] + s1[2 * x + 1]), inside, None, w2)
     v[0] = jnp.zeros((ROWS, CZ), F32)
     v[WX - 1] = jnp.zeros((ROWS, CZ), F32)
-    vcycle(v.at[pl.ds(1, BX)], r0, dp1_0, w0, dp1_1, w1, w2, e1, g1, e2, g2, band)
+    vcycle(v.at[pl.ds(1, BX)], r0, dp1_0, w0, dp1_1, w1, w2, e1, g1, e2, g2, tmp, band.at[pl.ds(0, 2 * CZ)])
     send_x(idx, v, out_a, out_b)
 
 
@@ -307,11 +318,12 @@
 
 
 def next_kernel(
-    idx, vin, xa, xb, ya, yb, rin, dp1_0, w0, dp1_1, w1, w2,
+    idx, vin, xa, xb, ya, yb, rin, dp1_0, w0, dp1_1, w1, w2, band,
     z, r, v, out_a, out_b,
-    w, got, e1, g1, e2, g2, band,
+    w, got, e1, g1, e2, g2, tmp,
 ):
     assemble(idx, w, vin, xa, xb, ya, yb, got)
+    clear_ends(tmp)
     z[...] = w[pl.ds(3, CX)]
 
     def emit(x, total):
@@ -319,11 +331,10 @@
             image = dp1_0[x - 1] * w[x] - total
             r[x - 1] = rin[x - 1] - (STEP * box_mask(idx, x - 1)) * image
 
-    wide_stencil(WX, w, band_matrix(3, 1), emit)
-    band[...] = band_matrix(2, 1)
+    stencil(WX, w, band, emit)
     v[0] = jnp.zeros((ROWS, CZ), F32)
     v[WX - 1] = jnp.zeros((ROWS, CZ), F32)
-    vcycle(v.at[pl.ds(1, BX)], r, dp1_0, w0, dp1_1, w1, w2, e1, g1, e2, g2, band)
+    vcycle(v.at[pl.ds(1, BX)], r, dp1_0, w0, dp1_1, w1, w2, e1, g1, e2, g2, tmp, band.at[pl.ds(0, 2 * CZ)])
     send_x(idx, v, out_a, out_b)
 
 
@@ -341,40 +352,30 @@
     return jnp.where((row >= 3) & (row < 3 + CY), 1.0, 0.0)
 
 
-def early_kernel(z0, z1, r0, r1, r2, sums):
-    own = own_rows()
-    acc = [jnp.zeros((ROWS, CZ), F32) for _ in range(5)]
-    for x in range(CX):
-        a0, a1 = z0[x] * own, z1[x] * own
-        b0, b1, b2 = r0[x + 2], r1[x + 2], r2[x + 2]
-        terms = (a0 * b0, a0 * b1, a0 * b2, a1 * b1, a1 * b2)
-        acc = [s + t for s, t in zip(acc, terms)]
-    sums[...] = jnp.broadcast_to(lane_sums([acc[0] * 0.0] * 2 + acc), sums.shape)
-
-
-def dots_kernel(idx, vin, xa, xb, ya, yb, dp1_0, r2, early, z2, u2, sums, w, got):
+def dots_kernel(idx, vin, xa, xb, ya, yb, dp1_0, z0, z1, r0, r1, r2, band, z2, u2, sums, w, got):
     assemble(idx, w, vin, xa, xb, ya, yb, got)
     own = own_rows()
-    acc = [jnp.zeros((ROWS, CZ), F32) for _ in range(2)]
+    acc = [jnp.zeros((ROWS, CZ), F32) for _ in range(7)]
 
     def emit(x, total):
         if 3 <= x < 3 + CX:
-            here = w[x]
-            image = dp1_0[x - 1] * here - total
-            z2[x - 3] = here
+            a2 = w[x]
+            image = dp1_0[x - 1] * a2 - total
+            z2[x - 3] = a2
             u2[x - 3] = image
-            here = here * own
-            acc[0] = acc[0] + here * r2[x - 1]
-            acc[1] = acc[1] + here * image
-
-    wide_stencil(WX, w, band_matrix(3, 1), emit)
-    sums[...] = jnp.broadcast_to(early[0:1, :] + lane_sums(acc), sums.shape)
-
-
-def final_kernel(gathered, z0, z1, z2, r0, r1, r2, u2, x_out, r_out):
+            a0, a1, a2 = z0[x - 3] * own, z1[x - 3] * own, a2 * own
+            b0, b1, b2 = r0[x - 1], r1[x - 1], r2[x - 1]
+            terms = (a0 * b0, a0 * b1, a0 * b2, a1 * b1, a1 * b2, a2 * b2, a2 * image)
+            acc[:] = [s + t for s, t in zip(acc, terms)]
+
+    stencil(WX, w, band, emit)
+    sums[...] = jnp.broadcast_to(lane_sums(acc), sums.shape)
+
+
+def final_kernel(gathered, z0, z1, z2, r0, r1, r2, u2, x_out, r_out, x_part, r_part, sems):
     row = jnp.sum(gathered[...], axis=0, keepdims=True)
     lane = lax.broadcasted_iota(jnp.int32, (1, CZ), 1)
-    m22, h22, m00, m01, m02, m11, m12 = (
+    m00, m01, m02, m11, m12, m22, h22 = (
         jnp.sum(jnp.where(lane == k, row, 0.0), axis=1, keepdims=True) for k in range(7)
     )
     inv = 1.0 / STEP
@@ -391,19 +392,28 @@
     c1 = y1 / d1 - l21 * c2
     c0 = m00 / h00 - l10 * c1 - l20 * c2
     f0, f1 = inv * c0, inv * c1
+    copies = []
     for x in range(CX):
         xs = c0 * z0[x] + c1 * z1[x] + c2 * z2[x]
         b0, b1 = r0[x + 2], r1[x + 2]
         rs = b0 - f0 * (b0 - b1) - f1 * (b1 - r2[x + 2]) - c2 * u2[x]
-        x_out[x] = xs[3 : 3 + CY, :]
-        r_out[x] = rs[3 : 3 + CY, :]
-
-
-def vmem(n):
-    return [pl.BlockSpec(memory_space=pltpu.VMEM) for _ in range(n)]
-
-
-def call(body, n_in, outs, scratch=(), smem=True, space=pltpu.VMEM):
+        x_part[x] = xs[3 : 3 + CY, :]
+        r_part[x] = rs[3 : 3 + CY, :]
+        if x % CHUNK == CHUNK - 1:
+            part = pl.ds(x + 1 - CHUNK, CHUNK)
+            for src, dst in ((x_part, x_out), (r_part, r_out)):
+                copies.append(
+                    pltpu.make_async_copy(src.at[part], dst.at[part], sems.at[len(copies)])
+                )
+                copies[-1].start()
+    for copy in copies:
+        copy.wait()
+
+
+CHUNK = 4
+
+
+def call(body, n_in, outs, scratch=(), smem=True, space=pltpu.VMEM, out=pltpu.VMEM):
     in_specs = [pl.BlockSpec(memory_space=space) for _ in range(n_in)]
     kernel = body
     if smem:
@@ -415,7 +425,7 @@
         kernel,
         out_shape=outs,
         in_specs=in_specs,
-        out_specs=vmem(len(outs)),
+        out_specs=[pl.BlockSpec(memory_space=out) for _ in outs],
         scratch_shapes=[pltpu.VMEM(s, F32) if isinstance(s, tuple) else s for s in scratch],
         interpret=INTERPRET,
         compiler_params=pltpu.CompilerParams(vmem_limit_bytes=VMEM_LIMIT),
@@ -459,12 +469,12 @@
         return a, b
 
     box = sds(BX, ROWS, CZ)
-    half = sds(BX // 2, ROWS, CZ)
-    quarter = sds(BX // 4, ROWS, CZ)
+    half = sds(BX // 2, CROWS, CZ)
+    quarter = sds(BX // 4, CROWS, CZ)
+    weights = [sds(2, BX, ROWS, CZ), half, sds(2, BX // 2, CROWS, CZ), sds(2, BX // 4, CROWS, CZ)]
     wide = sds(WX, ROWS, CZ)
     own = sds(CX, ROWS, CZ)
-    band = pltpu.VMEM((2 * CZ, CZ), jnp.bfloat16)
-    coarse = [half.shape, half.shape, quarter.shape, quarter.shape, band]
+    coarse = [half.shape, half.shape, quarter.shape, quarter.shape, (BX // 2, ROWS + 16, CZ)]
 
     def yrows(width):
         return -(-(CX - 4 + 2 * width) * width // 8) * 8
@@ -474,44 +484,45 @@
             width = xa.shape[0]
             xa, xb = swap_x(xa, xb)
             size = yrows(width)
-            ya, yb = call(
-                pack_y_kernel, 3, [sds(size, CZ)] * 2, [(WX, 16, CZ), (2, size, CZ)]
-            )(v, xa, xb)
+            ya, yb = call(pack_y_kernel, 3, [sds(size, CZ)] * 2, [(WX, 16, CZ), (2, size, CZ)])(v, xa, xb)
             return (v, xa, xb) + swap_y(ya, yb)
 
+        matrix = jnp.asarray(lane_matrix())
         first = sds(2, 2, CY, CZ)
         xa, xb = call(
             pack_x_kernel, 2, [first, first], [pltpu.SemaphoreType.DMA((4,))], space=pltpu.HBM
         )(*(pltpu.with_memory_space_constraint(a, pltpu.HBM) for a in (right_side, shift)))
         xa, xb = swap_x(xa, xb)
         strip = sds(IROWS, CZ)
-        rbox, sbox, ya, yb = call(
-            box_kernel, 4, [box, box, strip, strip], [(2, IROWS, CZ)]
-        )(right_side, shift, xa, xb)
+        rbox, sbox, ya, yb = call(box_kernel, 4, [box, box, strip, strip], [(2, IROWS, CZ)])(right_side, shift, xa, xb)
         ya, yb = swap_y(ya, yb)
         r0, v, xa, xb, *coefs = call(
             first_kernel,
-            4,
-            [box, wide, sds(5, ROWS, CZ), sds(5, ROWS, CZ), box, box, half, half, quarter],
+            5,
+            [box, wide, sds(5, ROWS, CZ), sds(5, ROWS, CZ), box] + weights,
             [(2, IROWS, CZ), box.shape, half.shape] + coarse,
-        )(rbox, sbox, ya, yb)
+        )(rbox, sbox, ya, yb, matrix)
         residuals, images = [r0], []
         for width in (5, 3):
             z, r, v, xa, xb = call(
                 next_kernel,
-                11,
+                12,
                 [own, box, wide, sds(width, ROWS, CZ), sds(width, ROWS, CZ)],
                 [wide.shape, (2, yrows(5), CZ)] + coarse,
-            )(*exchange(v, xa, xb), residuals[-1], *coefs)
+            )(*exchange(v, xa, xb), residuals[-1], *coefs, matrix)
             images.append(z)
             residuals.append(r)
-        early = call(early_kernel, 5, [sds(8, CZ)], smem=False)(*images, *residuals)[0]
         z2, u2, sums = call(
-            dots_kernel, 8, [own, own, sds(n_gx * n_gy, CZ)], [wide.shape, (2, yrows(3), CZ)]
-        )(*exchange(v, xa, xb), coefs[0], residuals[-1], early)
+            dots_kernel, 12, [own, own, sds(n_gx * n_gy, CZ)], [wide.shape, (2, yrows(3), CZ)]
+        )(*exchange(v, xa, xb), coefs[0], *images, *residuals, matrix)
         gathered = lax.all_to_all(sums, AX, 0, 0, tiled=True)
         x, r = call(
-            final_kernel, 8, [sds(CX, CY, CZ), sds(CX, CY, CZ)], smem=False
+            final_kernel,
+            8,
+            [sds(CX, CY, CZ)] * 2,
+            [(CX, CY, CZ), (CX, CY, CZ), pltpu.SemaphoreType.DMA((2 * CX // CHUNK,))],
+            smem=False,
+            out=pltpu.HBM,
         )(gathered, *images, z2, *residuals, u2)
         return x, r
 

time: 92.5 us -> 91.9 us (level)
    pallas_call x6 -> x5, Pallas kernels: 10 us -> 9.38 us  [the longest x2 5.35 us: on_device(): call(next_kernel, 12, [own, box, wide, sds(width, ROWS, CZ), sds(width, R...]
where the time goes in v1:
time: 91.9 us; the launch traced here: 91.7 us
  blocking collectives  55.4 us (60%)
  starting transfers between devices  24.9 us (27%)
  Pallas kernels  10.6 us (12%)
    all_to_all x1, blocking collectives, on_device(): gathered = lax.all_to_all(sums, AX, 0, 0, tiled=True)  22 us
    ppermute x4, starting transfers between devices, swap_y(): a = lax.ppermute(a, AX, pairs(n_gx, n_gy, 1, 0))  21.1 us
    all_gather x4, blocking collectives, swap_x(): lax.all_gather(b, AX, axis_index_groups=neighbours)  18.5 us
    all_gather x4, blocking collectives, swap_y(): b = lax.all_gather(b, AX, axis_index_groups=far)  14.9 us
    pallas_call x2, Pallas kernels, on_device(): call(next_kernel, 12, [own, box, wide, sds(width, ROWS, CZ), sds(width, R...  5.35 us
    ppermute x4, starting transfers between devices, swap_x(): lax.ppermute(a, AX, pairs(n_gx, n_gy, 0, 0))  3.83 us
    pallas_call x1, Pallas kernels, on_device(): call(first_kernel, 5, [box, wide, sds(5, ROWS, CZ), sds(5, ROWS, CZ), box...  2.33 us
  transfers between devices with their start and end apart: 8, of which 0 were waited for; matrix products, arithmetic and copies ran while one was open for 0% of the time, Pallas kernels for 0%

profile of v1, /device:TPU:1, one launch (start us, length us, event | category | flops | bytes accessed | tf_op | source)
XLA Modules:
  0.0 91.7 jit_solution(12239131601015918090)
XLA Ops:
  0.6 0.9 shard_map.50
  1.6 1.5 %collective-permute-start = (f32[2,2,32,128]{3,2,1,0:T(8,128)S(1)}, f32[2,2,32,128]{3,2,1,0:T(8,128)S(1)}, u32[]{:S(2)}, u32[]{:S(2)}) collective-permute-start(f32[2,2,32,128]{3,2,1,0:T(8,128)S(1)} %get-tuple-element.36), channel_id=1, source_target_pairs={{0,8},{1,9},{2,10},{3,11},{4,12},{5,13},{6,14},{7,15},{8,0},{9,1},... | collective-permute-start | bytes 196616 | tf_op jit(solution)/shard_map/ppermute | solution.py:462
  3.0 4.7 %all-gather = f32[4,2,32,128]{3,2,1,0:T(8,128)S(1)} all-gather(f32[2,2,32,128]{3,2,1,0:T(8,128)S(1)} %get-tuple-element.37), channel_id=2, replica_groups={{8,16},{9,17},{10,18},{11,19},{12,20},{13,21},{14,22},{15,23},{24,32},{..., dimensions={0}, use_global_device_ids=true | all-gather | bytes 196608 | tf_op jit(solution)/shard_map/all_gather | solution.py:463
  7.7 0.1 shard_map.51
  7.8 2.6 %collective-permute-start.1 = (f32[80,128]{1,0:T(8,128)S(1)}, f32[80,128]{1,0:T(8,128)S(1)}, u32[]{:S(2)}, u32[]{:S(2)}) collective-permute-start(f32[80,128]{1,0:T(8,128)S(1)} %get-tuple-element.40), channel_id=1, source_target_pairs={{0,1},{1,0},{2,3},{3,2},{4,5},{5,4},{6,7},{7,6},{8,9},{9,8},{10,11... | collective-permute-start | bytes 122888 | tf_op jit(solution)/shard_map/ppermute | solution.py:467
  10.5 3.9 %all-gather.1 = f32[160,128]{1,0:T(8,128)S(1)} all-gather(f32[80,128]{1,0:T(8,128)S(1)} %get-tuple-element.41), channel_id=3, replica_groups={{1,2},{3,4},{5,6},{9,10},{11,12},{13,14},{17,18},{19,20},{21,22},{25,26..., dimensions={0}, use_global_device_ids=true | all-gather | bytes 122880 | tf_op jit(solution)/shard_map/all_gather | solution.py:468
  14.4 2.3 %shard_map.52 = (f32[20,40,128]{2,1,0:T(8,128)S(1)}, f32[22,40,128]{2,1,0:T(8,128)S(1)}, f32[5,40,128]{2,1,0:T(8,128)S(1)}, f32[5,40,128]{2,1,0:T(8,128)S(1)}, f...) custom-call(f32[20,40,128]{2,1,0:T(8,128)S(1)} %get-tuple-element.38, ...), custom_call_target="tpu_custom_call" | custom-call | tf_op jit(solution)/shard_map/pallas_call | solution.py:499
  16.7 0.9 %collective-permute-start.2 = (f32[5,40,128]{2,1,0:T(8,128)S(1)}, f32[5,40,128]{2,1,0:T(8,128)S(1)}, u32[]{:S(2)}, u32[]{:S(2)}) collective-permute-start(f32[5,40,128]{2,1,0:T(8,128)S(1)} %get-tuple-element.43), channel_id=1, source_target_pairs={{0,8},{1,9},{2,10},{3,11},{4,12},{5,13},{6,14},{7,15},{8,0},{9,1},... | collective-permute-start | bytes 307208 | tf_op jit(solution)/shard_map/ppermute | solution.py:462
  17.7 4.8 %all-gather.2 = f32[10,40,128]{2,1,0:T(8,128)S(1)} all-gather(f32[5,40,128]{2,1,0:T(8,128)S(1)} %get-tuple-element.44), channel_id=4, replica_groups={{8,16},{9,17},{10,18},{11,19},{12,20},{13,21},{14,22},{15,23},{24,32},{..., dimensions={0}, use_global_device_ids=true | all-gather | bytes 307200 | tf_op jit(solution)/shard_map/all_gather | solution.py:463
  22.5 5.2 %collective-permute-start.3 = (f32[112,128]{1,0:T(8,128)S(1)}, f32[112,128]{1,0:T(8,128)S(1)}, u32[]{:S(2)}, u32[]{:S(2)}) collective-permute-start(f32[112,128]{1,0:T(8,128)S(1)} %get-tuple-element.45), channel_id=1, source_target_pairs={{0,1},{1,0},{2,3},{3,2},{4,5},{5,4},{6,7},{7,6},{8,9},{9,8},{10,11... | collective-permute-start | bytes 172040 | tf_op jit(solution)/shard_map/ppermute | solution.py:467
  27.7 3.6 %all-gather.3 = f32[224,128]{1,0:T(8,128)S(1)} all-gather(f32[112,128]{1,0:T(8,128)S(1)} %get-tuple-element.46), channel_id=5, replica_groups={{1,2},{3,4},{5,6},{9,10},{11,12},{13,14},{17,18},{19,20},{21,22},{25,26..., dimensions={0}, use_global_device_ids=true | all-gather | bytes 172032 | tf_op jit(solution)/shard_map/all_gather | solution.py:468
  31.3 2.7 %shard_map.54 = (f32[16,40,128]{2,1,0:T(8,128)S(1)}, f32[20,40,128]{2,1,0:T(8,128)S(1)}, f32[22,40,128]{2,1,0:T(8,128)S(1)}, f32[5,40,128]{2,1,0:T(8,128)S(1)}, f32[5,40,128]{2,1,0:T(8,128)S(1)}) custom-call(f32[22,40,128]{2,1,0:T(8,128)S(1)} %get-tuple-element.42.refs_0_, f32[5,40,128]{2,1,0:T(8,128)S(1)} %collective-permute-done.2.refs_1_, ...), custom_call_target="tpu_custom_call" | custom-call | tf_op jit(solution)/shard_map/pallas_call | solution.py:507
  33.9 0.7 collective-permute-start.4
  34.7 4.8 %all-gather.4 = f32[10,40,128]{2,1,0:T(8,128)S(1)} all-gather(f32[5,40,128]{2,1,0:T(8,128)S(1)} %get-tuple-element.55), channel_id=6, replica_groups={{8,16},{9,17},{10,18},{11,19},{12,20},{13,21},{14,22},{15,23},{24,32},{..., dimensions={0}, use_global_device_ids=true | all-gather | bytes 307200 | tf_op jit(solution)/shard_map/all_gather | solution.py:463
  39.5 5.4 %collective-permute-start.5 = (f32[112,128]{1,0:T(8,128)S(1)}, f32[112,128]{1,0:T(8,128)S(1)}, u32[]{:S(2)}, u32[]{:S(2)}) collective-permute-start(f32[112,128]{1,0:T(8,128)S(1)} %get-tuple-element.56), channel_id=1, source_target_pairs={{0,1},{1,0},{2,3},{3,2},{4,5},{5,4},{6,7},{7,6},{8,9},{9,8},{10,11... | collective-permute-start | bytes 172040 | tf_op jit(solution)/shard_map/ppermute | solution.py:467
  44.9 3.6 %all-gather.5 = f32[224,128]{1,0:T(8,128)S(1)} all-gather(f32[112,128]{1,0:T(8,128)S(1)} %get-tuple-element.57), channel_id=7, replica_groups={{1,2},{3,4},{5,6},{9,10},{11,12},{13,14},{17,18},{19,20},{21,22},{25,26..., dimensions={0}, use_global_device_ids=true | all-gather | bytes 172032 | tf_op jit(solution)/shard_map/all_gather | solution.py:468
  48.5 2.7 %shard_map.56 = (f32[16,40,128]{2,1,0:T(8,128)S(1)}, f32[20,40,128]{2,1,0:T(8,128)S(1)}, f32[22,40,128]{2,1,0:T(8,128)S(1)}, f32[3,40,128]{2,1,0:T(8,128)S(1)}, f32[3,40,128]{2,1,0:T(8,128)S(1)}) custom-call(f32[22,40,128]{2,1,0:T(8,128)S(1)} %get-tuple-element.53.refs_0_, f32[5,40,128]{2,1,0:T(8,128)S(1)} %collective-permute-done.4.refs_1_, ...), custom_call_target="tpu_custom_call" | custom-call | tf_op jit(solution)/shard_map/pallas_call | solution.py:507
  51.2 0.7 collective-permute-start.6
  51.9 4.3 %all-gather.6 = f32[6,40,128]{2,1,0:T(8,128)S(1)} all-gather(f32[3,40,128]{2,1,0:T(8,128)S(1)} %get-tuple-element.61), channel_id=8, replica_groups={{8,16},{9,17},{10,18},{11,19},{12,20},{13,21},{14,22},{15,23},{24,32},{..., dimensions={0}, use_global_device_ids=true | all-gather | bytes 184320 | tf_op jit(solution)/shard_map/all_gather | solution.py:463
  56.2 7.9 %collective-permute-start.7 = (f32[56,128]{1,0:T(8,128)S(1)}, f32[56,128]{1,0:T(8,128)S(1)}, u32[]{:S(2)}, u32[]{:S(2)}) collective-permute-start(f32[56,128]{1,0:T(8,128)S(1)} %get-tuple-element.62), channel_id=1, source_target_pairs={{0,1},{1,0},{2,3},{3,2},{4,5},{5,4},{6,7},{7,6},{8,9},{9,8},{10,11... | collective-permute-start | bytes 86024 | tf_op jit(solution)/shard_map/ppermute | solution.py:467
  64.1 3.9 %all-gather.7 = f32[112,128]{1,0:T(8,128)S(1)} all-gather(f32[56,128]{1,0:T(8,128)S(1)} %get-tuple-element.63), channel_id=9, replica_groups={{1,2},{3,4},{5,6},{9,10},{11,12},{13,14},{17,18},{19,20},{21,22},{25,26..., dimensions={0}, use_global_device_ids=true | all-gather | bytes 86016 | tf_op jit(solution)/shard_map/all_gather | solution.py:468
  68.0 0.7 shard_map.58
  68.7 22.0 %all_to_all.11 = f32[128,1,128]{2,1,0:T(1,128)S(1)} all-to-all(f32[128,1,128]{2,1,0:T(1,128)S(1)} %bitcast.24), channel_id=1, replica_groups=mesh['gx'=16,'gy'=8] {'gx','gy'}, dimensions={0} | all-to-all | bytes 131072 | tf_op jit(solution)/shard_map/all_to_all | solution.py:518
  90.7 1.0 %shard_map.59 = (f32[16,32,128]{2,1,0:T(8,128)}, f32[16,32,128]{2,1,0:T(8,128)}) custom-call(f32[128,128]{1,0:T(8,128)S(1)} %bitcast.22, f32[16,40,128]{2,1,0:T(8,128)S(1)} %get-tuple-element.64.refs_6_.z0, f32[16,40,128]{2,1,0:T(8,128)S(1)} %get-tuple-element.65.refs_7_.z1, f32[16,40,128]{2,1,0:T(8,128)S(1)} %get-tuple-element.68.z2, ...), custom_call_target="tpu_custom_call" | custom-call | tf_op jit(solution)/shard_map/pallas_call | solution.py:519
  (17 shorter events, 0.2 us)
Async XLA Ops:
  0.6 7.1 %copy-start.2 = (f32[16,32,128]{2,1,0:T(8,128)S(1)}, f32[16,32,128]{2,1,0:T(8,128)}, u32[]{:S(2)}) copy-start(f32[16,32,128]{2,1,0:T(8,128)} %refs_1_.3) | copy-start | bytes 786436
  0.6 7.0 %copy-start.1 = (f32[16,32,128]{2,1,0:T(8,128)S(1)}, f32[16,32,128]{2,1,0:T(8,128)}, u32[]{:S(2)}) copy-start(f32[16,32,128]{2,1,0:T(8,128)} %refs_0_.3) | copy-start | bytes 786436
  1.6 6.1 %collective-permute-start = (f32[2,2,32,128]{3,2,1,0:T(8,128)S(1)}, f32[2,2,32,128]{3,2,1,0:T(8,128)S(1)}, u32[]{:S(2)}, u32[]{:S(2)}) collective-permute-start(f32[2,2,32,128]{3,2,1,0:T(8,128)S(1)} %get-tuple-element.36), channel_id=1, source_target_pairs={{0,8},{1,9},{2,10},{3,11},{4,12},{5,13},{6,14},{7,15},{8,0},{9,1},... | collective-permute-start | bytes 196616 | tf_op jit(solution)/shard_map/ppermute | solution.py:462
  7.8 6.5 %copy-start = (bf16[384,128]{1,0:T(8,128)(2,1)S(1)}, bf16[384,128]{1,0:T(8,128)(2,1)}, u32[]{:S(2)}) copy-start(bf16[384,128]{1,0:T(8,128)(2,1)} %constant.2.clone.refs_4_.refs_11_) | copy-start | bytes 294916
  7.8 6.5 %collective-permute-start.1 = (f32[80,128]{1,0:T(8,128)S(1)}, f32[80,128]{1,0:T(8,128)S(1)}, u32[]{:S(2)}, u32[]{:S(2)}) collective-permute-start(f32[80,128]{1,0:T(8,128)S(1)} %get-tuple-element.40), channel_id=1, source_target_pairs={{0,1},{1,0},{2,3},{3,2},{4,5},{5,4},{6,7},{7,6},{8,9},{9,8},{10,11... | collective-permute-start | bytes 122888 | tf_op jit(solution)/shard_map/ppermute | solution.py:467
  16.7 5.7 %collective-permute-start.2 = (f32[5,40,128]{2,1,0:T(8,128)S(1)}, f32[5,40,128]{2,1,0:T(8,128)S(1)}, u32[]{:S(2)}, u32[]{:S(2)}) collective-permute-start(f32[5,40,128]{2,1,0:T(8,128)S(1)} %get-tuple-element.43), channel_id=1, source_target_pairs={{0,8},{1,9},{2,10},{3,11},{4,12},{5,13},{6,14},{7,15},{8,0},{9,1},... | collective-permute-start | bytes 307208 | tf_op jit(solution)/shard_map/ppermute | solution.py:462
  22.5 8.8 %collective-permute-start.3 = (f32[112,128]{1,0:T(8,128)S(1)}, f32[112,128]{1,0:T(8,128)S(1)}, u32[]{:S(2)}, u32[]{:S(2)}) collective-permute-start(f32[112,128]{1,0:T(8,128)S(1)} %get-tuple-element.45), channel_id=1, source_target_pairs={{0,1},{1,0},{2,3},{3,2},{4,5},{5,4},{6,7},{7,6},{8,9},{9,8},{10,11... | collective-permute-start | bytes 172040 | tf_op jit(solution)/shard_map/ppermute | solution.py:467
  33.9 5.5 %collective-permute-start.4 = (f32[5,40,128]{2,1,0:T(8,128)S(1)}, f32[5,40,128]{2,1,0:T(8,128)S(1)}, u32[]{:S(2)}, u32[]{:S(2)}) collective-permute-start(f32[5,40,128]{2,1,0:T(8,128)S(1)} %get-tuple-element.54), channel_id=1, source_target_pairs={{0,8},{1,9},{2,10},{3,11},{4,12},{5,13},{6,14},{7,15},{8,0},{9,1},... | collective-permute-start | bytes 307208 | tf_op jit(solution)/shard_map/ppermute | solution.py:462
  39.5 9.0 %collective-permute-start.5 = (f32[112,128]{1,0:T(8,128)S(1)}, f32[112,128]{1,0:T(8,128)S(1)}, u32[]{:S(2)}, u32[]{:S(2)}) collective-permute-start(f32[112,128]{1,0:T(8,128)S(1)} %get-tuple-element.56), channel_id=1, source_target_pairs={{0,1},{1,0},{2,3},{3,2},{4,5},{5,4},{6,7},{7,6},{8,9},{9,8},{10,11... | collective-permute-start | bytes 172040 | tf_op jit(solution)/shard_map/ppermute | solution.py:467
  51.2 5.0 %collective-permute-start.6 = (f32[3,40,128]{2,1,0:T(8,128)S(1)}, f32[3,40,128]{2,1,0:T(8,128)S(1)}, u32[]{:S(2)}, u32[]{:S(2)}) collective-permute-start(f32[3,40,128]{2,1,0:T(8,128)S(1)} %get-tuple-element.60), channel_id=1, source_target_pairs={{0,8},{1,9},{2,10},{3,11},{4,12},{5,13},{6,14},{7,15},{8,0},{9,1},... | collective-permute-start | bytes 184328 | tf_op jit(solution)/shard_map/ppermute | solution.py:462
  56.2 11.8 %collective-permute-start.7 = (f32[56,128]{1,0:T(8,128)S(1)}, f32[56,128]{1,0:T(8,128)S(1)}, u32[]{:S(2)}, u32[]{:S(2)}) collective-permute-start(f32[56,128]{1,0:T(8,128)S(1)} %get-tuple-element.62), channel_id=1, source_target_pairs={{0,1},{1,0},{2,3},{3,2},{4,5},{5,4},{6,7},{7,6},{8,9},{9,8},{10,11... | collective-permute-start | bytes 86024 | tf_op jit(solution)/shard_map/ppermute | solution.py:467
